TPU v7x, 32 devices: a whole 2x2x4 slice. The times are simulated.
32 devices in a mesh: grp: 2 (over y), kvp: 4 (over z), tp: 4 (over x, core).
Axes of the slice: x: 2, y: 2, z: 4, core: 2. Of those that a mesh axis runs over, the one named last changes fastest.
Arguments:
- queries: bfloat16 [32, 4096], P('grp', 'tp'), parts along dimension 0, may hold values from -6 to 6
- keys: bfloat16 [32, 512, 512], P('grp', 'kvp', 'tp'), parts along dimension 0, may hold values from -6 to 6
- values: bfloat16 [32, 512, 512], P('grp', 'kvp', 'tp'), parts along dimension 0, may hold values from -6 to 6
- lengths: int32 [32], P('grp'), parts along dimension 0, may hold values from 256 to 512, as said below
- out_weight: bfloat16 [4096, 1536], P('tp', 'kvp'), may hold values from -0.375 to 0.375
- residual: bfloat16 [32, 1536], P('grp', 'kvp'), parts along dimension 0, may hold values from -20 to 20
- norm_gain: bfloat16 [1536], P('kvp'), may hold values from 0.099609375 to 1.8984375
- expert_ids: int32 [32, 4], P('grp'), parts along dimension 0, may hold values from 0 to 3, as said below
- gate_probs: float32 [32, 4], P('grp'), parts along dimension 0, may hold values from 0.2 to 1
- w_gate: bfloat16 [4, 1536, 1536], P('kvp', None, 'tp'), may hold values from -0.15625 to 0.15625
- w_up: bfloat16 [4, 1536, 1536], P('kvp', None, 'tp'), may hold values from -0.15625 to 0.15625
- w_down: bfloat16 [4, 1536, 1536], P('kvp', 'tp'), may hold values from -0.15625 to 0.15625
Outputs:
- attended: float32 [32, 4096], P('grp', 'tp'), parts along dimension 0
- mixed: bfloat16 [32, 1536], P('grp', 'kvp'), parts along dimension 0
There are 2 independent parts, one for each index of `grp`. A program takes and returns all parts, laid end to end along the dimension named above; an argument that names none is the same for every part. Nothing has to cross between parts.
Inputs may be any that keep to these rules, and one draw needn't show every extreme that they name: `lengths`: at least one sequence has all 512 positions valid. `expert_ids`: each row names 4 different experts; no expert is named by more than 16 rows, and some expert by exactly 16.
All inputs are finite; a program needn't handle non-finite values.
Results may differ from a plain program's by a relative error of at most 0.006.
Values may be sent and summed in bfloat16 or wider, within the bound.
No kernel may reach another device: no remote copies, remote signals or barrier semaphores. Data moves between devices by JAX's collectives and lax.ppermute only.
A program may use at most 64 MiB of HBM per device.

v0:
```python
import jax
import jax.numpy as jnp
from jax import lax
from jax.sharding import PartitionSpec as P

D = 1536
HEAD = 64
EPSILON = 1e-05
NEGATIVE = -1e30


def merged(part, axis, combine):
    gathered = jax.tree.map(lambda a: lax.all_gather(a, axis), part)

    def take(source):
        return jax.tree.map(lambda a: lax.dynamic_index_in_dim(a, source, 0, False), gathered)

    return lax.fori_loop(
        1, lax.axis_size(axis), lambda source, state: combine(state, take(source)), take(0)
    )


def slot_tables(expert_ids, gate_probs, experts, capacity):
    batch_size, top_count = expert_ids.shape
    flat_ids = expert_ids.reshape(-1)
    pair_count = flat_ids.shape[0]
    pair_order = jnp.arange(pair_count, dtype=jnp.int32)
    earlier_same = (flat_ids[:, None] == flat_ids[None, :]) & (
        pair_order[None, :] < pair_order[:, None]
    )
    slot_index = jnp.sum(earlier_same.astype(jnp.int32), axis=1)
    target_col = flat_ids * capacity + slot_index
    columns = jnp.arange(experts * capacity, dtype=jnp.int32)
    hit_table = (target_col[:, None] == columns[None, :]).astype(jnp.float32)
    hit_table = hit_table.reshape(batch_size, top_count, experts * capacity)
    dispatch = jnp.sum(hit_table, axis=1)
    combine = jnp.sum(hit_table * gate_probs[:, :, None], axis=1)
    return (dispatch, combine)


def merge_partial(earlier, latest):
    global_max = jnp.maximum(earlier[0], latest[0])
    lead_scale = jnp.exp(earlier[0] - global_max)
    trail_scale = jnp.exp(latest[0] - global_max)
    return (
        global_max,
        lead_scale * earlier[1] + trail_scale * latest[1],
        lead_scale[..., None] * earlier[2] + trail_scale[..., None] * latest[2],
    )


def on_device(
    queries,
    keys,
    values,
    lengths,
    out_weight,
    residual,
    norm_gain,
    expert_ids,
    gate_probs,
    w_gate,
    w_up,
    w_down,
):
    batch_size = queries.shape[0]
    local_kv = keys.shape[2] // HEAD
    local_heads = queries.shape[1] // HEAD
    group_size = local_heads // local_kv
    ctx_dev = keys.shape[1]
    shards = lax.axis_size("kvp")
    query_heads = queries.reshape(batch_size, local_kv, group_size, HEAD)
    key_rows = keys.reshape(batch_size, ctx_dev, local_kv, HEAD)
    value_rows = values.reshape(batch_size, ctx_dev, local_kv, HEAD)
    scores = jnp.einsum(
        "bgrd,bcgd->bgrc", query_heads, key_rows, preferred_element_type=jnp.float32
    ) * HEAD ** (-0.5)
    position = lax.axis_index("kvp") * ctx_dev + jnp.arange(ctx_dev, dtype=jnp.int32)
    valid_key = (position[None, :] < lengths[:, None])[:, None, None, :]
    masked = jnp.where(valid_key, scores, NEGATIVE)
    block_max = jnp.max(masked, axis=3)
    weights = jnp.where(valid_key, jnp.exp(masked - block_max[..., None]), 0.0)
    rounded = weights.astype(jnp.bfloat16)
    block_sum = jnp.sum(rounded.astype(jnp.float32), axis=3)
    block_out = jnp.einsum(
        "bgrc,bcgd->bgrd", rounded, value_rows, preferred_element_type=jnp.float32
    )
    global_max, denominator, summed = merged(
        (block_max, block_sum, block_out), "kvp", merge_partial
    )
    attended = (summed / denominator[..., None]).reshape(batch_size, local_heads * HEAD)
    projected = lax.psum(
        jnp.dot(attended.astype(jnp.bfloat16), out_weight, preferred_element_type=jnp.float32), "tp"
    )
    hidden_state = lax.optimization_barrier(
        (projected + residual.astype(jnp.float32)).astype(jnp.bfloat16)
    )
    state_wide = hidden_state.astype(jnp.float32)
    col_count = hidden_state.shape[1]
    exp_dev = w_gate.shape[0]
    experts = exp_dev * shards
    capacity = min(batch_size, max(2, 2 * batch_size * expert_ids.shape[1] // experts))
    dispatch, combine = slot_tables(expert_ids, gate_probs, experts, capacity)
    total_sq = lax.psum(jnp.sum(state_wide * state_wide, axis=1), "kvp")
    inverse = lax.rsqrt(total_sq / D + EPSILON)
    normed = (state_wide * inverse[:, None] * norm_gain.astype(jnp.float32)[None, :]).astype(
        jnp.bfloat16
    )
    outgoing = jnp.dot(
        dispatch.T.astype(jnp.bfloat16), normed, preferred_element_type=jnp.float32
    ).astype(jnp.bfloat16)
    outgoing = outgoing.reshape(experts, capacity, col_count)
    expert_rows = lax.all_to_all(outgoing, "kvp", split_axis=0, concat_axis=2, tiled=True)
    gate_proj = jnp.einsum("ecd,edf->ecf", expert_rows, w_gate, preferred_element_type=jnp.float32)
    up_proj = jnp.einsum("ecd,edf->ecf", expert_rows, w_up, preferred_element_type=jnp.float32)
    activation = (jax.nn.silu(gate_proj) * up_proj).astype(jnp.bfloat16)
    partial_value = jnp.einsum(
        "ecf,efd->ecd", activation, w_down, preferred_element_type=jnp.float32
    )
    returned = lax.all_to_all(partial_value, "kvp", split_axis=2, concat_axis=0, tiled=True)
    moe_local = jnp.dot(
        combine, returned.reshape(experts * capacity, col_count), precision=lax.Precision.HIGHEST
    )
    moe_term = lax.psum(moe_local, "tp")
    mixed = (state_wide + moe_term).astype(jnp.bfloat16)
    return (attended, mixed)


def solution(mesh):
    return jax.shard_map(
        on_device,
        mesh=mesh,
        in_specs=(
            P("grp", "tp"),
            P("grp", "kvp", "tp"),
            P("grp", "kvp", "tp"),
            P("grp"),
            P("tp", "kvp"),
            P("grp", "kvp"),
            P("kvp"),
            P("grp", None),
            P("grp", None),
            P("kvp", None, "tp"),
            P("kvp", None, "tp"),
            P("kvp", "tp", None),
        ),
        out_specs=(P("grp", "tp"), P("grp", "kvp")),
        check_vma=False,
    )
```

profile of v0, /device:TPU:0, one launch (start us, length us, event | category | flops | bytes accessed | tf_op | source)
XLA Modules:
  0.0 124.9 jit_solution(10427162739778779653)
XLA Ops:
  0.6 0.0 copy-start
  0.6 0.0 copy-start.5
  0.7 0.8 convert_element_type.54
  1.4 0.8 copy.99
  2.2 0.1 eq.13
  2.3 0.2 convert_reduce_fusion.2
  2.5 0.1 reduce_sum.49
  2.6 0.1 copy.100
  2.6 1.3 %multiply_add_fusion = s32[16,4]{0,1:T(4,128)} fusion(s32[16,4]{0,1:T(4,128)S(1)} %copy.100, s32[16,4]{0,1:T(4,128)} %param.21), kind=kLoop, calls=%fused_computation.48 | loop fusion | flops 128 | bytes 768 | tf_op jit(solution)/shard_map/add | solution.py:32
  3.9 0.9 reshape.104
  4.8 0.0 copy-start.3
  4.8 1.4 %copy.90 = bf16[16,128,128]{1,2,0:T(8,128)(2,1)S(1)} copy(bf16[16,128,128]{2,1,0:T(8,128)(2,1)} %param.15) | data formatting | bytes 1048576 | tf_op args[1]
  6.2 0.0 copy-done.5
  6.2 0.1 broadcast_compare_fusion
  6.3 0.3 fusion.39
  6.6 14.9 %all-gather = f32[64,2,8]{2,1,0:T(2,128)S(1)} all-gather(f32[16,2,8]{2,1,0:T(2,128)S(1)} %get-tuple-element.236), channel_id=2, replica_groups=mesh['grp'=2,'kvp'=4,'tp'=4] {'kvp'}, dimensions={0}, use_global_device_ids=true | all-gather | bytes 5120 | tf_op jit(solution)/shard_map/all_gather | solution.py:13
  21.5 0.2 convert_reduce_fusion
  21.7 13.3 %all-gather.1 = f32[64,2,8]{2,1,0:T(2,128)S(1)} all-gather(f32[16,2,8]{2,1,0:T(2,128)S(1)} %convert_reduce_fusion), channel_id=3, replica_groups=mesh['grp'=2,'kvp'=4,'tp'=4] {'kvp'}, dimensions={0}, use_global_device_ids=true | all-gather | bytes 5120 | tf_op jit(solution)/shard_map/all_gather | solution.py:13
  35.1 0.1 copy.95
  35.1 0.1 copy.97
  35.2 0.1 copy.94
  35.3 0.1 copy.96
  35.4 0.0 copy-done.3
  35.4 0.3 copy.91
  35.7 0.4 fusion.35
  36.1 15.1 %all-gather.2 = f32[64,2,8,64]{3,2,1,0:T(8,128)S(1)} all-gather(f32[16,2,8,64]{3,2,1,0:T(8,128)S(1)} %fusion.35), channel_id=4, replica_groups=mesh['grp'=2,'kvp'=4,'tp'=4] {'kvp'}, dimensions={0}, use_global_device_ids=true | all-gather | bytes 327680 | tf_op jit(solution)/shard_map/all_gather | solution.py:13
  51.3 1.1 while.19
  51.3 0.1 copy.113
  51.4 0.1 copy.114
  51.5 0.2 fusion.53
  51.7 0.1 copy.113
  51.8 0.1 copy.114
  51.9 0.2 fusion.53
  52.1 0.1 copy.113
  52.2 0.1 copy.114
  52.2 0.2 fusion.53
  52.4 0.0 copy-start.2
  52.4 0.1 copy.98
  52.5 0.1 broadcast_divide_fusion
  52.6 0.7 reshape.107
  53.4 2.1 %fusion.18 = f32[16,384]{1,0:T(8,128)} fusion(bf16[1024,384]{1,0:T(8,128)(2,1)} %param.18, f32[16,1024]{1,0:T(8,128)} %reshape.107), kind=kOutput, calls=%fused_computation.30 | convolution fusion | flops 12599296 | bytes 876544 | tf_op jit(solution)/shard_map/dot_general | solution.py:93
  55.4 11.4 %psum.21 = f32[16,384]{1,0:T(8,128)} all-reduce(f32[16,384]{1,0:T(8,128)} %fusion.18), channel_id=1, replica_groups=mesh['grp'=2,'kvp'=4,'tp'=4] {'tp'}, use_global_device_ids=true, to_apply=%region_4.5 | all-reduce | flops 6144 | bytes 49152 | tf_op jit(solution)/shard_map/psum | solution.py:92
  66.8 0.7 add_convert_fusion
  67.5 0.6 fusion.21
  68.2 12.5 %psum.22 = f32[16]{0:T(128)} all-reduce(f32[16]{0:T(128)} %fusion.21), channel_id=1, replica_groups=mesh['grp'=2,'kvp'=4,'tp'=4] {'kvp'}, use_global_device_ids=true, to_apply=%region_9.10 | all-reduce | flops 16 | bytes 128 | tf_op jit(solution)/shard_map/psum | solution.py:104
  80.7 0.7 add_rsqrt_fusion
  81.4 1.4 %convert_reduce_fusion.1 = (bf16[16,64]{1,0:T(8,128)(2,1)S(1)}, f32[16,64]{1,0:T(8,128)}) fusion(s32[16,4]{0,1:T(4,128)} %multiply_add_fusion, f32[16,4]{0,1:T(4,128)} %param.22), kind=kLoop, calls=%fused_computation.25 | loop fusion | flops 18432 | bytes 6656 | tf_op jit(solution)/shard_map/reduce_sum | solution.py:36
  82.7 0.2 convolution_convert_fusion
  82.9 8.1 %all_to_all.30 = bf16[4,16,384]{2,1,0:T(8,128)(2,1)S(1)} all-to-all(bf16[4,16,384]{2,1,0:T(8,128)(2,1)S(1)} %bitcast.73), channel_id=1, replica_groups=mesh['grp'=2,'kvp'=4,'tp'=4] {'kvp'}, dimensions={0} | all-to-all | bytes 98304 | tf_op jit(solution)/shard_map/all_to_all | solution.py:113
  91.0 0.6 copy.110
  91.6 1.7 %fusion.7 = f32[16,384]{1,0:T(8,128)} fusion(bf16[16,1536]{1,0:T(8,128)(2,1)} %bitcast.23, bf16[1,1536,384]{2,1,0:T(8,128)(2,1)S(1)} %copy-done.2), kind=kOutput, calls=%fused_computation.12 | convolution fusion | flops 18874368 | bytes 1253376 | tf_op jit(solution)/shard_map/ecd,edf->ecf/dot_general | solution.py:114
  93.3 1.6 %fusion.3 = f32[16,1536]{0,1:T(8,128)S(1)} fusion(bf16[1,384,1536]{2,1,0:T(8,128)(2,1)S(1)} %copy-done, bf16[16,1536]{1,0:T(8,128)(2,1)} %bitcast.23, bf16[1,1536,384]{2,1,0:T(8,128)(2,1)S(1)} %copy-done.1, f32[16,384]{1,0:T(8,128)} %fusion.7), kind=kOutput, calls=%fused_computation.8 | convolution fusion | flops 37785600 | bytes 2531328 | tf_op jit(solution)/shard_map/ecf,efd->ecd/dot_general | solution.py:117
  95.0 0.6 broadcast.55
  95.6 7.2 %reduce = f32[1536,16]{1,0:T(8,128)S(1)} reduce(f32[1536,1,16]{2,1,0:T(1,128)S(1)} %bitcast.66, f32[]{:T(128)} %broadcast.55), dimensions={1}, to_apply=%bitcast.47.reduce_sub_computation | reduce | bytes 196612
  102.8 0.3 reshape.123
  103.1 0.0 copy-start.4
  103.1 8.2 %all_to_all.31 = f32[4,1,6144]{2,1,0:T(1,128)S(1)} all-to-all(f32[4,1,6144]{2,1,0:T(1,128)S(1)} %reshape.123), channel_id=1, replica_groups=mesh['grp'=2,'kvp'=4,'tp'=4] {'kvp'}, dimensions={0} | all-to-all | bytes 196608 | tf_op jit(solution)/shard_map/all_to_all | solution.py:120
  111.3 0.9 reduce.1
  112.3 1.3 %reshape.124 = f32[1536,1,16]{2,1,0:T(1,128)S(1)} reshape(f32[4,6144]{1,0:T(4,128)S(1)} %reduce.1) | data formatting | bytes 196608
  113.6 0.2 copy.109
  113.9 0.0 copy-done.4
  113.9 0.2 fusion.40
  114.0 10.3 %psum.23 = f32[16,384]{1,0:T(8,128)S(1)} all-reduce(f32[16,384]{1,0:T(8,128)S(1)} %fusion.40), channel_id=1, replica_groups=mesh['grp'=2,'kvp'=4,'tp'=4] {'tp'}, use_global_device_ids=true, to_apply=%region_10.11 | all-reduce | flops 6144 | bytes 49152 | tf_op jit(solution)/shard_map/psum | solution.py:124
  124.3 0.6 fusion.24
  (13 shorter events, 0.1 us)
Async XLA Ops:
  0.6 92.7 %copy-start = (bf16[1,384,1536]{2,1,0:T(8,128)(2,1)S(1)}, bf16[1,384,1536]{2,1,0:T(8,128)(2,1)}, u32[]{:S(2)}) copy-start(bf16[1,384,1536]{2,1,0:T(8,128)(2,1)} %param.25) | copy-start | bytes 3538948
  0.6 5.5 %copy-start.5 = (s32[16]{0:T(128)S(1)}, s32[16]{0:T(128)}, u32[]{:S(2)}) copy-start(s32[16]{0:T(128)} %param.17) | copy-start | bytes 196
  4.8 30.6 %copy-start.3 = (bf16[16,128,128]{2,1,0:T(8,128)(2,1)S(1)}, bf16[16,128,128]{2,1,0:T(8,128)(2,1)}, u32[]{:S(2)}) copy-start(bf16[16,128,128]{2,1,0:T(8,128)(2,1)} %param.16) | copy-start | bytes 1572868
  52.4 39.2 %copy-start.2 = (bf16[1,1536,384]{2,1,0:T(8,128)(2,1)S(1)}, bf16[1,1536,384]{2,1,0:T(8,128)(2,1)}, u32[]{:S(2)}) copy-start(bf16[1,1536,384]{2,1,0:T(8,128)(2,1)} %param.23) | copy-start | bytes 3538948
  53.4 40.0 %copy-start.1 = (bf16[1,1536,384]{2,1,0:T(8,128)(2,1)S(1)}, bf16[1,1536,384]{2,1,0:T(8,128)(2,1)}, u32[]{:S(2)}) copy-start(bf16[1,1536,384]{2,1,0:T(8,128)(2,1)} %param.24) | copy-start | bytes 3538948
  103.1 10.8 %copy-start.4 = (f32[16,64]{1,0:T(8,128)S(1)}, f32[16,64]{1,0:T(8,128)}, u32[]{:S(2)}) copy-start(f32[16,64]{1,0:T(8,128)} %get-tuple-element.217) | copy-start | bytes 12292
where the time goes:
time: 126 us; the launch traced here: 125 us
  blocking collectives  93.8 us (74%)
  other arithmetic  15.3 us (12%)
  local copies, waits for them, and re-layouts  8.31 us (7%)
  matrix products  6.53 us (5%)
    all_gather x3, blocking collectives, merged(): gathered = jax.tree.map(lambda a: lax.all_gather(a, axis), part)  43.4 us
    psum x1, blocking collectives, on_device(): total_sq = lax.psum(jnp.sum(state_wide * state_wide, axis=1), 'kvp')  12.5 us
    psum x1, blocking collectives, on_device(): lax.psum(jnp.dot(attended.astype(jnp.bfloat16), out_weight, preferred_ele...  11.4 us
    psum x1, blocking collectives, on_device(): moe_term = lax.psum(moe_local, 'tp')  10.3 us
    all_to_all x1, blocking collectives, on_device(): lax.all_to_all(partial_value, 'kvp', split_axis=2, concat_axis=0, tiled=T...  8.21 us
    all_to_all x1, blocking collectives, on_device(): lax.all_to_all(outgoing, 'kvp', split_axis=0, concat_axis=2, tiled=True)  8.06 us
    unnamed x1, other arithmetic  7.21 us
    unnamed x19, local copies, waits for them, and re-layouts  5.3 us

commit v1 on v0

--- a/solution.py
+++ b/solution.py
@@ -7,6 +7,15 @@
 HEAD = 64
 EPSILON = 1e-05
 NEGATIVE = -1e30
+
+
+def added_up(x, axis):
+    count = lax.axis_size(axis)
+    total, stride = (x, 1)
+    while stride < count:
+        total = total + lax.ppermute(total, axis, [(i, i ^ stride) for i in range(count)])
+        stride = 2 * stride
+    return total
 
 
 def merged(part, axis, combine):
@@ -121,7 +130,7 @@
     moe_local = jnp.dot(
         combine, returned.reshape(experts * capacity, col_count), precision=lax.Precision.HIGHEST
     )
-    moe_term = lax.psum(moe_local, "tp")
+    moe_term = added_up(moe_local, "tp")
     mixed = (state_wide + moe_term).astype(jnp.bfloat16)
     return (attended, mixed)
 

time: 126 us -> 120 us (0.952)
  blocking collectives: 93.8 us -> 83.5 us
  waiting for transfers between devices: 0 us -> 3.26 us
  starting transfers between devices: 0 us -> 1.81 us
    psum x1 -> x0, blocking collectives: 10.3 us -> none  [on_device(): moe_term = lax.psum(moe_local, 'tp')]
    ppermute x0 -> x2, waiting for transfers between devices: none -> 3.26 us  [added_up(): lax.ppermute(total, axis, [(i, i ^ stride) for i in range(count)])]
    ppermute x0 -> x2, starting transfers between devices: none -> 1.81 us  [added_up(): lax.ppermute(total, axis, [(i, i ^ stride) for i in range(count)])]
  transfers between devices with their start and end apart: 0 -> 2, of which waited for: 0 -> 2; matrix products, arithmetic and copies ran while one was open for 0% -> 0% of each run, Pallas kernels for 0% -> 0%
where the time goes in v1:
time: 120 us
  blocking collectives  83.5 us (70%)
  other arithmetic  15.4 us (13%)
  local copies, waits for them, and re-layouts  8.31 us (7%)
  matrix products  6.53 us (5%)
  waiting for transfers between devices  3.26 us (3%)
  starting transfers between devices  1.81 us (2%)
    all_gather x3, blocking collectives, merged(): gathered = jax.tree.map(lambda a: lax.all_gather(a, axis), part)  43.4 us
    psum x1, blocking collectives, on_device(): total_sq = lax.psum(jnp.sum(state_wide * state_wide, axis=1), 'kvp')  12.5 us
    psum x1, blocking collectives, on_device(): lax.psum(jnp.dot(attended.astype(jnp.bfloat16), out_weight, preferred_ele...  11.4 us
    all_to_all x1, blocking collectives, on_device(): lax.all_to_all(partial_value, 'kvp', split_axis=2, concat_axis=0, tiled=T...  8.21 us
    all_to_all x1, blocking collectives, on_device(): lax.all_to_all(outgoing, 'kvp', split_axis=0, concat_axis=2, tiled=True)  8.06 us
    unnamed x1, other arithmetic  7.21 us
    unnamed x19, local copies, waits for them, and re-layouts  5.3 us
    ppermute x2, waiting for transfers between devices, added_up(): lax.ppermute(total, axis, [(i, i ^ stride) for i in range(count)])  3.26 us
  transfers between devices with their start and end apart: 2, of which 2 were waited for; matrix products, arithmetic and copies ran while one was open for 0% of the time, Pallas kernels for 0%

profile of v1, /device:TPU:0, one launch (start us, length us, event | category | flops | bytes accessed | tf_op | source)
XLA Modules:
  0.0 119.7 jit_solution(7369977174813172955)
XLA Ops:
  0.6 0.0 copy-start
  0.7 0.8 convert_element_type.54
  1.4 0.8 copy.99
  2.2 0.1 eq.13
  2.3 0.2 convert_reduce_fusion.2
  2.5 0.1 reduce_sum.49
  2.6 0.1 copy.100
  2.6 1.3 %multiply_add_fusion = s32[16,4]{0,1:T(4,128)} fusion(s32[16,4]{0,1:T(4,128)S(1)} %copy.100, s32[16,4]{0,1:T(4,128)} %param.21), kind=kLoop, calls=%fused_computation.48 | loop fusion | flops 128 | bytes 768 | tf_op jit(solution)/shard_map/add | solution.py:41
  3.9 0.9 reshape.104
  4.8 0.0 copy-start.3
  4.8 1.4 %copy.90 = bf16[16,128,128]{1,2,0:T(8,128)(2,1)S(1)} copy(bf16[16,128,128]{2,1,0:T(8,128)(2,1)} %param.15) | data formatting | bytes 1048576 | tf_op args[1]
  6.2 0.1 broadcast_compare_fusion
  6.3 0.3 fusion.39
  6.6 14.9 %all-gather = f32[64,2,8]{2,1,0:T(2,128)S(1)} all-gather(f32[16,2,8]{2,1,0:T(2,128)S(1)} %get-tuple-element.236), channel_id=2, replica_groups=mesh['grp'=2,'kvp'=4,'tp'=4] {'kvp'}, dimensions={0}, use_global_device_ids=true | all-gather | bytes 5120 | tf_op jit(solution)/shard_map/all_gather | solution.py:22
  21.5 0.2 convert_reduce_fusion
  21.7 13.3 %all-gather.1 = f32[64,2,8]{2,1,0:T(2,128)S(1)} all-gather(f32[16,2,8]{2,1,0:T(2,128)S(1)} %convert_reduce_fusion), channel_id=3, replica_groups=mesh['grp'=2,'kvp'=4,'tp'=4] {'kvp'}, dimensions={0}, use_global_device_ids=true | all-gather | bytes 5120 | tf_op jit(solution)/shard_map/all_gather | solution.py:22
  35.1 0.1 copy.95
  35.1 0.1 copy.97
  35.2 0.1 copy.94
  35.3 0.1 copy.96
  35.4 0.3 copy.91
  35.7 0.4 fusion.35
  36.1 15.1 %all-gather.2 = f32[64,2,8,64]{3,2,1,0:T(8,128)S(1)} all-gather(f32[16,2,8,64]{3,2,1,0:T(8,128)S(1)} %fusion.35), channel_id=4, replica_groups=mesh['grp'=2,'kvp'=4,'tp'=4] {'kvp'}, dimensions={0}, use_global_device_ids=true | all-gather | bytes 327680 | tf_op jit(solution)/shard_map/all_gather | solution.py:22
  51.3 1.1 while.19
  51.3 0.1 copy.113
  51.4 0.1 copy.114
  51.5 0.2 fusion.53
  51.7 0.1 copy.113
  51.8 0.1 copy.114
  51.9 0.2 fusion.53
  52.1 0.1 copy.113
  52.2 0.1 copy.114
  52.2 0.2 fusion.53
  52.4 0.0 copy-start.2
  52.4 0.1 copy.98
  52.5 0.1 broadcast_divide_fusion
  52.6 0.7 reshape.107
  53.4 2.1 %fusion.18 = f32[16,384]{1,0:T(8,128)} fusion(bf16[1024,384]{1,0:T(8,128)(2,1)} %param.18, f32[16,1024]{1,0:T(8,128)} %reshape.107), kind=kOutput, calls=%fused_computation.30 | convolution fusion | flops 12599296 | bytes 876544 | tf_op jit(solution)/shard_map/dot_general | solution.py:102
  55.4 11.4 %psum.14 = f32[16,384]{1,0:T(8,128)} all-reduce(f32[16,384]{1,0:T(8,128)} %fusion.18), channel_id=1, replica_groups=mesh['grp'=2,'kvp'=4,'tp'=4] {'tp'}, use_global_device_ids=true, to_apply=%region_4.5 | all-reduce | flops 6144 | bytes 49152 | tf_op jit(solution)/shard_map/psum | solution.py:101
  66.8 0.7 add_convert_fusion
  67.5 0.6 fusion.21
  68.2 12.5 %psum.15 = f32[16]{0:T(128)} all-reduce(f32[16]{0:T(128)} %fusion.21), channel_id=1, replica_groups=mesh['grp'=2,'kvp'=4,'tp'=4] {'kvp'}, use_global_device_ids=true, to_apply=%region_9.10 | all-reduce | flops 16 | bytes 128 | tf_op jit(solution)/shard_map/psum | solution.py:113
  80.7 0.7 add_rsqrt_fusion
  81.4 1.4 %convert_reduce_fusion.1 = (bf16[16,64]{1,0:T(8,128)(2,1)S(1)}, f32[16,64]{1,0:T(8,128)}) fusion(s32[16,4]{0,1:T(4,128)} %multiply_add_fusion, f32[16,4]{0,1:T(4,128)} %param.22), kind=kLoop, calls=%fused_computation.25 | loop fusion | flops 18432 | bytes 6656 | tf_op jit(solution)/shard_map/reduce_sum | solution.py:45
  82.7 0.2 convolution_convert_fusion
  82.9 8.1 %all_to_all.30 = bf16[4,16,384]{2,1,0:T(8,128)(2,1)S(1)} all-to-all(bf16[4,16,384]{2,1,0:T(8,128)(2,1)S(1)} %bitcast.73), channel_id=1, replica_groups=mesh['grp'=2,'kvp'=4,'tp'=4] {'kvp'}, dimensions={0} | all-to-all | bytes 98304 | tf_op jit(solution)/shard_map/all_to_all | solution.py:122
  91.0 0.6 copy.110
  91.6 1.7 %fusion.7 = f32[16,384]{1,0:T(8,128)} fusion(bf16[16,1536]{1,0:T(8,128)(2,1)} %bitcast.23, bf16[1,1536,384]{2,1,0:T(8,128)(2,1)S(1)} %copy-done.2), kind=kOutput, calls=%fused_computation.12 | convolution fusion | flops 18874368 | bytes 1253376 | tf_op jit(solution)/shard_map/ecd,edf->ecf/dot_general | solution.py:123
  93.3 1.6 %fusion.3 = f32[16,1536]{0,1:T(8,128)S(1)} fusion(bf16[1,384,1536]{2,1,0:T(8,128)(2,1)S(1)} %copy-done, bf16[16,1536]{1,0:T(8,128)(2,1)} %bitcast.23, bf16[1,1536,384]{2,1,0:T(8,128)(2,1)S(1)} %copy-done.1, f32[16,384]{1,0:T(8,128)} %fusion.7), kind=kOutput, calls=%fused_computation.8 | convolution fusion | flops 37785600 | bytes 2531328 | tf_op jit(solution)/shard_map/ecf,efd->ecd/dot_general | solution.py:126
  95.0 0.6 broadcast.55
  95.6 7.2 %reduce = f32[1536,16]{1,0:T(8,128)S(1)} reduce(f32[1536,1,16]{2,1,0:T(1,128)S(1)} %bitcast.66, f32[]{:T(128)} %broadcast.55), dimensions={1}, to_apply=%bitcast.47.reduce_sub_computation | reduce | bytes 196612
  102.8 0.3 reshape.123
  103.1 0.0 copy-start.4
  103.1 8.2 %all_to_all.31 = f32[4,1,6144]{2,1,0:T(1,128)S(1)} all-to-all(f32[4,1,6144]{2,1,0:T(1,128)S(1)} %reshape.123), channel_id=1, replica_groups=mesh['grp'=2,'kvp'=4,'tp'=4] {'kvp'}, dimensions={0} | all-to-all | bytes 196608 | tf_op jit(solution)/shard_map/all_to_all | solution.py:129
  111.3 0.9 reduce.1
  112.3 1.3 %reshape.124 = f32[1536,1,16]{2,1,0:T(1,128)S(1)} reshape(f32[4,6144]{1,0:T(4,128)S(1)} %reduce.1) | data formatting | bytes 196608
  113.6 0.2 copy.109
  113.9 0.0 copy-done.4
  113.9 0.2 fusion.40
  114.0 0.1 collective-permute-start
  114.1 1.2 collective-permute-done
  115.3 1.7 %collective-permute-start.1 = (f32[16,384]{1,0:T(8,128)S(1)}, f32[16,384]{1,0:T(8,128)S(1)}, u32[]{:S(2)}, u32[]{:S(2)}) collective-permute-start(f32[16,384]{1,0:T(8,128)S(1)} %add.107), channel_id=1, source_target_pairs={{0,2},{1,3},{2,0},{3,1},{4,6},{5,7},{6,4},{7,5},{8,10},{9,11},{10,... | collective-permute-start | bytes 73736 | tf_op jit(solution)/shard_map/ppermute | solution.py:16
  117.0 2.1 %collective-permute-done.1 = f32[16,384]{1,0:T(8,128)S(1)} collective-permute-done((f32[16,384]{1,0:T(8,128)S(1)}, f32[16,384]{1,0:T(8,128)S(1)}, u32[]{:S(2)}, u32[]{:S(2)}) %collective-permute-start.1) | collective-permute-done | bytes 24608 | tf_op jit(solution)/shard_map/ppermute | solution.py:16
  119.1 0.6 fusion.24
  (17 shorter events, 0.1 us)
Async XLA Ops:
  0.6 92.7 %copy-start = (bf16[1,384,1536]{2,1,0:T(8,128)(2,1)S(1)}, bf16[1,384,1536]{2,1,0:T(8,128)(2,1)}, u32[]{:S(2)}) copy-start(bf16[1,384,1536]{2,1,0:T(8,128)(2,1)} %param.25) | copy-start | bytes 3538948
  0.6 5.5 %copy-start.5 = (s32[16]{0:T(128)S(1)}, s32[16]{0:T(128)}, u32[]{:S(2)}) copy-start(s32[16]{0:T(128)} %param.17) | copy-start | bytes 196
  4.8 30.6 %copy-start.3 = (bf16[16,128,128]{2,1,0:T(8,128)(2,1)S(1)}, bf16[16,128,128]{2,1,0:T(8,128)(2,1)}, u32[]{:S(2)}) copy-start(bf16[16,128,128]{2,1,0:T(8,128)(2,1)} %param.16) | copy-start | bytes 1572868
  52.4 39.2 %copy-start.2 = (bf16[1,1536,384]{2,1,0:T(8,128)(2,1)S(1)}, bf16[1,1536,384]{2,1,0:T(8,128)(2,1)}, u32[]{:S(2)}) copy-start(bf16[1,1536,384]{2,1,0:T(8,128)(2,1)} %param.23) | copy-start | bytes 3538948
  53.4 40.0 %copy-start.1 = (bf16[1,1536,384]{2,1,0:T(8,128)(2,1)S(1)}, bf16[1,1536,384]{2,1,0:T(8,128)(2,1)}, u32[]{:S(2)}) copy-start(bf16[1,1536,384]{2,1,0:T(8,128)(2,1)} %param.24) | copy-start | bytes 3538948
  103.1 10.8 %copy-start.4 = (f32[16,64]{1,0:T(8,128)S(1)}, f32[16,64]{1,0:T(8,128)}, u32[]{:S(2)}) copy-start(f32[16,64]{1,0:T(8,128)} %get-tuple-element.217) | copy-start | bytes 12292
  114.0 1.3 %collective-permute-start = (f32[16,384]{1,0:T(8,128)S(1)}, f32[16,384]{1,0:T(8,128)S(1)}, u32[]{:S(2)}, u32[]{:S(2)}) collective-permute-start(f32[16,384]{1,0:T(8,128)S(1)} %fusion.40), channel_id=1, source_target_pairs={{0,1},{1,0},{2,3},{3,2},{4,5},{5,4},{6,7},{7,6},{8,9},{9,8},{10,11... | collective-permute-start | bytes 73736 | tf_op jit(solution)/shard_map/ppermute | solution.py:16
  115.3 3.8 %collective-permute-start.1 = (f32[16,384]{1,0:T(8,128)S(1)}, f32[16,384]{1,0:T(8,128)S(1)}, u32[]{:S(2)}, u32[]{:S(2)}) collective-permute-start(f32[16,384]{1,0:T(8,128)S(1)} %add.107), channel_id=1, source_target_pairs={{0,2},{1,3},{2,0},{3,1},{4,6},{5,7},{6,4},{7,5},{8,10},{9,11},{10,... | collective-permute-start | bytes 73736 | tf_op jit(solution)/shard_map/ppermute | solution.py:16
